TPU v7x, 32 devices: a whole 2x2x4 slice. The times are simulated.
32 devices in a mesh: dp: 16 (over z, y, x), mp: 2 (over core).
Axes of the slice: x: 2, y: 2, z: 4, core: 2. Of those that a mesh axis runs over, the one named last changes fastest.
Arguments:
- tokens: bfloat16 [32768, 768], P(('dp', 'mp')), may hold values from -6 to 6
- w_query: bfloat16 [768, 768], P('dp', 'mp'), may hold values from -0.625 to 0.625
- w_key: bfloat16 [768, 768], P('dp', 'mp'), may hold values from -0.625 to 0.625
- w_value: bfloat16 [768, 768], P('dp', 'mp'), may hold values from -0.21875 to 0.21875
- value_taps: float32 [12, 33], P('mp'), may hold values from -0.3 to 0.3
- w_output: bfloat16 [768, 768], P(None, ('dp', 'mp')), may hold values from -0.875 to 0.875
- first_gain: bfloat16 [768], P(('dp', 'mp')), may hold values from 0.25 to 1.75
- first_bias: bfloat16 [768], P(('dp', 'mp')), may hold values from -1.5 to 1.5
- w_expand: bfloat16 [768, 3072], P('dp', 'mp'), may hold values from -0.21875 to 0.21875
- w_shrink: bfloat16 [3072, 768], P('mp', 'dp'), may hold values from -0.21875 to 0.21875
- second_gain: bfloat16 [768], P(('dp', 'mp')), may hold values from 0.25 to 1.75
- second_bias: bfloat16 [768], P(('dp', 'mp')), may hold values from -1.5 to 1.5
- doc_lengths: int32 [32], replicated, may hold values from 256 to 1024, as said below
- out_grad: bfloat16 [32768, 768], P(('dp', 'mp')), may hold values from -6 to 6
Outputs:
- layer_out: bfloat16 [32768, 768], P(('dp', 'mp'))
- tokens_grad: float32 [32768, 768], P(('dp', 'mp'))
- query_grad: float32 [768, 768], P('dp', 'mp')
- key_grad: float32 [768, 768], P('dp', 'mp')
- value_grad: float32 [768, 768], P('dp', 'mp')
- taps_grad: float32 [12, 33], P('mp')
- output_grad: float32 [768, 768], P(None, ('dp', 'mp'))
- first_gain_grad: float32 [768], P(('dp', 'mp'))
- first_bias_grad: float32 [768], P(('dp', 'mp'))
- expand_grad: float32 [768, 3072], P('dp', 'mp')
- shrink_grad: float32 [3072, 768], P('mp', 'dp')
- second_gain_grad: float32 [768], P(('dp', 'mp'))
- second_bias_grad: float32 [768], P(('dp', 'mp'))
Inputs may be any that keep to these rules, and one draw needn't show every extreme that they name: Document i occupies the first doc_lengths[i] positions of slot i of 1024 positions; the rest is padding. In every draw some document fills its whole slot.
All inputs are finite; a program needn't handle non-finite values.
Results may differ from a plain program's by a relative error of at most 0.018.
The roundings to bfloat16 on the way count: a program that leaves them out, or rounds other values in their place, can miss the bound.
Values may be sent and summed in bfloat16 or wider, within the bound.
A program may use at most 320 MiB of HBM per device.

v0:
```python
import jax
import jax.numpy as jnp
from jax import lax
from jax.sharding import PartitionSpec as P

HEAD_DIM = 64
LANDMARKS = 64
KERNEL = 33
PINV_STEPS = 6
HIGH = lax.Precision.HIGHEST


def ahead(left, right):
    return jnp.dot(left, right, preferred_element_type=jnp.float32)


def against(left, right):
    return lax.dot_general(
        left, right, (((1,), (1,)), ((), ())), preferred_element_type=jnp.float32
    )


def across(left, right):
    return lax.dot_general(
        left, right, (((0,), (0,)), ((), ())), preferred_element_type=jnp.float32
    )


def layer_norm(values, gain, bias):
    middle = jnp.mean(values, axis=-1, keepdims=True)
    centered = values - middle
    variance = jnp.mean(centered * centered, axis=-1, keepdims=True)
    return centered * lax.rsqrt(variance + 1e-05) * gain + bias


def exact_gelu(values):
    return jax.nn.gelu(values, approximate=False)


def inverse_estimate(matrix):
    widest = jnp.max(jnp.sum(matrix, axis=-2), axis=-1)
    current = jnp.swapaxes(matrix, -1, -2) / widest[:, None, None]
    identity = jnp.eye(matrix.shape[-1], dtype=jnp.float32)[None]
    for step in range(PINV_STEPS):
        product = jnp.einsum("hij,hjk->hik", matrix, current, precision=HIGH)
        inner_term = 7.0 * identity - product
        inner_term = 15.0 * identity - jnp.einsum(
            "hij,hjk->hik", product, inner_term, precision=HIGH
        )
        inner_term = 13.0 * identity - jnp.einsum(
            "hij,hjk->hik", product, inner_term, precision=HIGH
        )
        current = 0.25 * jnp.einsum("hij,hjk->hik", current, inner_term, precision=HIGH)
    return current


def nystrom(query, keys, values, taps, length):
    slots = query.shape[0]
    positions = jnp.arange(slots, dtype=jnp.int32)
    valid = positions < length
    weight = valid.astype(jnp.float32)
    segment = positions * LANDMARKS // length
    member = (
        (segment[None, :] == jnp.arange(LANDMARKS, dtype=jnp.int32)[:, None]) & valid[None, :]
    ).astype(jnp.float32)
    member = member / jnp.sum(member, axis=1, keepdims=True)
    mark_query = jnp.einsum("js,shd->hjd", member, query, precision=HIGH)
    mark_keys = jnp.einsum("js,shd->hjd", member, keys, precision=HIGH)
    scale = HEAD_DIM ** (-0.5)
    first = jax.nn.softmax(
        jnp.einsum("shd,hjd->hsj", query, mark_keys, precision=HIGH) * scale, axis=-1
    )
    second = jax.nn.softmax(
        jnp.einsum("hid,hjd->hij", mark_query, mark_keys, precision=HIGH) * scale, axis=-1
    )
    third_scores = jnp.einsum("hjd,shd->hjs", mark_query, keys, precision=HIGH) * scale
    third = jax.nn.softmax(jnp.where(valid[None, None, :], third_scores, -1e30), axis=-1)
    inverse = inverse_estimate(second)
    summary = jnp.einsum("hjs,shd->hjd", third, values, precision=HIGH)
    carried = jnp.einsum("hij,hjd->hid", inverse, summary, precision=HIGH)
    mixed = jnp.einsum("hsj,hjd->shd", first, carried, precision=HIGH)
    radius = KERNEL // 2
    padded = jnp.pad(values * weight[:, None, None], ((radius, radius), (0, 0), (0, 0)))
    for index in range(KERNEL):
        mixed = mixed + taps[:, index][None, :, None] * padded[index : index + slots]
    mixed = mixed * weight[:, None, None]
    return mixed.reshape(slots, query.shape[1] * HEAD_DIM)


def on_device(
    tokens,
    w_query,
    w_key,
    w_value,
    value_taps,
    w_output,
    first_gain,
    first_bias,
    w_expand,
    w_shrink,
    second_gain,
    second_bias,
    doc_lengths,
    out_grad,
):
    parts = lax.axis_size("mp")
    group = lax.axis_index("dp")
    slots = tokens.shape[0]
    pair = lax.dynamic_slice_in_dim(doc_lengths, group * parts, parts)
    full_query, full_keys, full_values, full_expand, full_shrink = (
        lax.all_gather(w_query, "dp", axis=0, tiled=True),
        lax.all_gather(w_key, "dp", axis=0, tiled=True),
        lax.all_gather(w_value, "dp", axis=0, tiled=True),
        lax.all_gather(w_expand, "dp", axis=0, tiled=True),
        lax.all_gather(w_shrink, "dp", axis=1, tiled=True),
    )
    full_output, gain_one, bias_one, gain_two, bias_two = (
        lax.all_gather(w_output, ("dp", "mp"), axis=1, tiled=True),
        lax.all_gather(first_gain, ("dp", "mp"), axis=0, tiled=True),
        lax.all_gather(first_bias, ("dp", "mp"), axis=0, tiled=True),
        lax.all_gather(second_gain, ("dp", "mp"), axis=0, tiled=True),
        lax.all_gather(second_bias, ("dp", "mp"), axis=0, tiled=True),
    )
    gain_one = gain_one.astype(jnp.float32)
    bias_one = bias_one.astype(jnp.float32)
    gain_two = gain_two.astype(jnp.float32)
    bias_two = bias_two.astype(jnp.float32)
    local_heads = full_query.shape[1] // HEAD_DIM
    grouped = lax.all_gather(tokens, "mp", axis=0, tiled=True)
    query_low = ahead(grouped, full_query).astype(jnp.bfloat16)
    keys_low = ahead(grouped, full_keys).astype(jnp.bfloat16)
    values_low = ahead(grouped, full_values).astype(jnp.bfloat16)

    def attention_core(query, keys, values, taps):
        shape = (parts, slots, local_heads, HEAD_DIM)
        mixed = jax.vmap(nystrom, in_axes=(0, 0, 0, None, 0))(
            query.reshape(shape), keys.reshape(shape), values.reshape(shape), taps, pair
        )
        return mixed.reshape(parts * slots, local_heads * HEAD_DIM)

    attended, core_back = jax.vjp(
        attention_core,
        query_low.astype(jnp.float32),
        keys_low.astype(jnp.float32),
        values_low.astype(jnp.float32),
        value_taps,
    )
    attended_tok = lax.all_to_all(
        attended.astype(jnp.bfloat16), "mp", split_axis=0, concat_axis=1, tiled=True
    )
    projected = ahead(attended_tok, full_output)
    first_out, first_back = jax.vjp(
        layer_norm, tokens.astype(jnp.float32) + projected, gain_one, bias_one
    )
    hidden_all = lax.all_gather(first_out.astype(jnp.bfloat16), "mp", axis=0, tiled=True)
    pre = ahead(hidden_all, full_expand)
    active, gelu_back = jax.vjp(exact_gelu, pre)
    active_low = active.astype(jnp.bfloat16)
    branch = lax.psum_scatter(
        ahead(active_low, full_shrink).astype(jnp.bfloat16), "mp", scatter_dimension=0, tiled=True
    ).astype(jnp.float32)
    result, second_back = jax.vjp(layer_norm, first_out + branch, gain_two, bias_two)
    layer_out = result.astype(jnp.bfloat16)
    d_second_in, gain_two_grad, bias_two_grad = second_back(out_grad.astype(jnp.float32))
    branch_grad = lax.all_gather(d_second_in.astype(jnp.bfloat16), "mp", axis=0, tiled=True)
    back_query, back_keys, back_values, back_expand, back_shrink = (
        lax.all_gather(w_query, "dp", axis=0, tiled=True),
        lax.all_gather(w_key, "dp", axis=0, tiled=True),
        lax.all_gather(w_value, "dp", axis=0, tiled=True),
        lax.all_gather(w_expand, "dp", axis=0, tiled=True),
        lax.all_gather(w_shrink, "dp", axis=1, tiled=True),
    )
    (d_pre,) = gelu_back(against(branch_grad, back_shrink))
    d_pre_low = d_pre.astype(jnp.bfloat16)
    shrink_grad = across(active_low, branch_grad)
    expand_grad = across(hidden_all, d_pre_low)
    d_hidden = lax.psum_scatter(
        against(d_pre_low, back_expand).astype(jnp.bfloat16), "mp", scatter_dimension=0, tiled=True
    ).astype(jnp.float32)
    d_first_in, gain_one_grad, bias_one_grad = first_back(d_second_in + d_hidden)
    d_projected = d_first_in.astype(jnp.bfloat16)
    output_grad = across(attended_tok, d_projected)
    d_attended = against(d_projected, full_output).astype(jnp.bfloat16)
    d_heads = lax.all_to_all(d_attended, "mp", split_axis=1, concat_axis=0, tiled=True)
    d_query, d_keys, d_values, taps_grad = core_back(d_heads.astype(jnp.float32))
    d_query = d_query.astype(jnp.bfloat16)
    d_keys = d_keys.astype(jnp.bfloat16)
    d_values = d_values.astype(jnp.bfloat16)
    query_grad = across(grouped, d_query)
    key_grad = across(grouped, d_keys)
    value_grad = across(grouped, d_values)
    total = against(d_query, back_query)
    total = total + against(d_keys, back_keys)
    tokens_grad = d_first_in + lax.psum_scatter(
        (total + against(d_values, back_values)).astype(jnp.bfloat16),
        "mp",
        scatter_dimension=0,
        tiled=True,
    ).astype(jnp.float32)
    query_grad, key_grad, value_grad, expand_grad, shrink_grad = (
        lax.psum_scatter(query_grad, "dp", scatter_dimension=0, tiled=True),
        lax.psum_scatter(key_grad, "dp", scatter_dimension=0, tiled=True),
        lax.psum_scatter(value_grad, "dp", scatter_dimension=0, tiled=True),
        lax.psum_scatter(expand_grad, "dp", scatter_dimension=0, tiled=True),
        lax.psum_scatter(shrink_grad, "dp", scatter_dimension=1, tiled=True),
    )
    output_grad, gain_one_grad, bias_one_grad, gain_two_grad, bias_two_grad = (
        lax.psum_scatter(output_grad, ("dp", "mp"), scatter_dimension=1, tiled=True),
        lax.psum_scatter(gain_one_grad, ("dp", "mp"), scatter_dimension=0, tiled=True),
        lax.psum_scatter(bias_one_grad, ("dp", "mp"), scatter_dimension=0, tiled=True),
        lax.psum_scatter(gain_two_grad, ("dp", "mp"), scatter_dimension=0, tiled=True),
        lax.psum_scatter(bias_two_grad, ("dp", "mp"), scatter_dimension=0, tiled=True),
    )
    taps_grad = lax.psum(taps_grad, "dp")
    return (
        layer_out,
        tokens_grad,
        query_grad,
        key_grad,
        value_grad,
        taps_grad,
        output_grad,
        gain_one_grad,
        bias_one_grad,
        expand_grad,
        shrink_grad,
        gain_two_grad,
        bias_two_grad,
    )


def solution(mesh):
    in_specs = (
        P(("dp", "mp"), None),
        P("dp", "mp"),
        P("dp", "mp"),
        P("dp", "mp"),
        P("mp", None),
        P(None, ("dp", "mp")),
        P(("dp", "mp")),
        P(("dp", "mp")),
        P("dp", "mp"),
        P("mp", "dp"),
        P(("dp", "mp")),
        P(("dp", "mp")),
        P(),
        P(("dp", "mp"), None),
    )
    out_specs = (
        P(("dp", "mp"), None),
        P(("dp", "mp"), None),
        P("dp", "mp"),
        P("dp", "mp"),
        P("dp", "mp"),
        P("mp", None),
        P(None, ("dp", "mp")),
        P(("dp", "mp")),
        P(("dp", "mp")),
        P("dp", "mp"),
        P("mp", "dp"),
        P(("dp", "mp")),
        P(("dp", "mp")),
    )
    return jax.shard_map(
        on_device, mesh=mesh, in_specs=in_specs, out_specs=out_specs, check_vma=False
    )
```

profile of v0, /device:TPU:0, one launch (start us, length us, event | category | flops | bytes accessed | tf_op | source)
XLA Modules:
  0.0 1484.3 jit_solution(6945524106746862283)
XLA Ops:
  18.9 42.1 %all-reduce.76 = (bf16[768]{0:T(1024)(128)(2,1)S(1)}, bf16[768]{0:T(1024)(128)(2,1)S(1)}, bf16[768]{0:T(1024)(128)(2,1)}, bf16[768]{0:T(1024)(128)(2,1)}) all-reduce(bf16[768]{0:T(1024)(128)(2,1)S(1)} %dynamic-update-slice.1, bf16[768]{0:T(1024)(128)(2,1)S(1)} %dynamic-update-slice, ...), channel_id=1, replica_groups=mesh['dp'=16,'mp'=2] {'dp','mp'}, use_global_device_ids=true, to_apply=%add.68 | all-reduce | flops 3072 | bytes 12288
  62.4 44.0 %all_gather.45 = bf16[768,384]{1,0:T(8,128)(2,1)S(1)} all-gather(bf16[48,384]{1,0:T(8,128)(2,1)S(1)} %copy-done.119), channel_id=1, replica_groups=mesh['dp'=16,'mp'=2] {'dp'}, dimensions={0}, use_global_device_ids=true | all-gather | bytes 626688 | tf_op jit(solution)/shard_map/all_gather | solution.py:111
  106.3 41.1 %all_gather.46 = bf16[768,384]{1,0:T(8,128)(2,1)S(1)} all-gather(bf16[48,384]{1,0:T(8,128)(2,1)S(1)} %copy-done.120), channel_id=1, replica_groups=mesh['dp'=16,'mp'=2] {'dp'}, dimensions={0}, use_global_device_ids=true | all-gather | bytes 626688 | tf_op jit(solution)/shard_map/all_gather | solution.py:112
  147.4 43.7 %all_gather.47 = bf16[768,384]{1,0:T(8,128)(2,1)} all-gather(bf16[48,384]{1,0:T(8,128)(2,1)S(1)} %copy-done.121), channel_id=1, replica_groups=mesh['dp'=16,'mp'=2] {'dp'}, dimensions={0}, use_global_device_ids=true | all-gather | bytes 626688 | tf_op jit(solution)/shard_map/all_gather | solution.py:113
  267.9 29.7 %multiply_convert_fusion.1 = bf16[2,1024,6,64]{1,3,2,0:T(8,128)(2,1)} fusion(f32[2,1024,6,64]{1,3,2,0:T(8,128)S(1)} %copy_multiply_fusion, f32[2,6,64,64]{3,2,1,0:T(8,128)S(1)} %fusion.157, f32[6]{0:T(128)S(1)} %copy-done.146, f32[6]{0:T(128)S(1)} %copy-done.156, f32[6]{0:T(128)S(1)} %copy-done.158, f32[6]{0:T(128)S(1)} %copy-done.160, ...), kind=kOutput, calls=%fused_computation.121 | convolution fusion | flops 659816448 | bytes 8168216 | tf_op jit(solution)/shard_map/jvp(vmap(hsj,hjd->shd))/dot_general | solution.py:81
  311.6 7.5 all-gather.11.cloned.1.call-done
  319.1 35.5 %multiply_convert_fusion = (bf16[2048,1536]{1,0:T(8,128)(2,1)}, f32[2048,1536]{1,0:T(8,128)}, f32[2048,1536]{1,0:T(8,128)}) fusion(bf16[2048,768]{0,1:T(8,128)(2,1)} %all-gather.11.cloned.1.call-done, bf16[768,1536]{1,0:T(8,128)(2,1)} %all-gather.13.cloned.1.call-done), kind=kOutput, calls=%fused_computation.3 | convolution fusion | flops 5036310528 | bytes 36962304 | tf_op jit(solution)/shard_map/dot_general | solution.py:14
  354.6 30.5 %all-gather.15.cloned.1.call-done = bf16[1536,768]{0,1:T(8,128)(2,1)} async-done(((bf16[1536,48]{0,1:T(8,128)(2,1)}), bf16[1536,768]{0,1:T(8,128)(2,1)}) %all-gather.15.cloned.1.call-update) | async-done | bytes 2359312 | tf_op jit(solution)/shard_map/all_gather | solution.py:115
  385.1 9.1 convolution_convert_fusion.1
  397.4 6.2 reduce-scatter.16.cloned.1.call-done
  415.1 13.5 all-gather.17.cloned.1.call-done
  428.6 17.3 %add_convert_fusion = bf16[2048,1536]{1,0:T(8,128)(2,1)S(1)} fusion(f32[2048,1536]{1,0:T(8,128)} %get-tuple-element.153, f32[2048,1536]{1,0:T(8,128)} %get-tuple-element.200, bf16[2048,768]{0,1:T(8,128)(2,1)} %all-gather.17.cloned.1.call-done, bf16[1536,768]{0,1:T(8,128)(2,1)} %all-gather.15.cloned.1.call-done), kind=kOutput, calls=%fused_computation.2 | convolution fusion | flops 4875878400 | bytes 36962304 | tf_op jit(solution)/shard_map/dot_general | solution.py:18
  448.6 6.4 convolution_convert_fusion
  459.4 8.0 reduce-scatter.18.cloned.1.call-done
  486.2 5.6 fusion.15
  534.2 15.2 %multiply_reduce_fusion.32 = (f32[6]{0:T(128)}, f32[6]{0:T(128)}, f32[6]{0:T(128)}, f32[6]{0:T(128)}, f32[6]{0:T(128)}, /*index=5*/f32[6]{0:T(128)}, f32[6]{0:T(...) fusion(f32[2,1024,6,64]{1,3,2,0:T(8,128)S(1)} %copy-done.5, ...), kind=kLoop, calls=%fused_computation.107 | loop fusion | flops 25952166 | bytes 12591512 | tf_op jit(solution)/shard_map/transpose(jvp(vmap()))/reduce_sum | solution.py:85
  549.6 16.9 %broadcast_multiply_fusion.1 = (f32[2,1024,6,64]{1,3,2,0:T(8,128)}, f32[2,1024,6,64]{1,3,2,0:T(8,128)}, f32[2,1024,6,64]{1,3,2,0:T(8,128)}, f32[2,1024,6,64]{1,3...) fusion(f32[6]{0:T(128)S(1)} %copy-done.157, ...), kind=kLoop, calls=%fused_computation.168 | loop fusion | flops 11796480 | bytes 47194448 | tf_op jit(solution)/shard_map/transpose(jvp(vmap()))/mul | solution.py:85
  566.5 21.3 %broadcast_multiply_fusion = (f32[2,1024,6,64]{1,3,2,0:T(8,128)}, f32[2,1024,6,64]{1,3,2,0:T(8,128)}, f32[2,1024,6,64]{1,3,2,0:T(8,128)}, f32[2,1024,6,64]{1,3,2...) fusion(f32[6]{0:T(128)} %get-tuple-element.134, ...), kind=kLoop, calls=%fused_computation.167 | loop fusion | flops 14155776 | bytes 56631704 | tf_op jit(solution)/shard_map/transpose(jvp(vmap()))/mul | solution.py:85
  630.5 34.7 %pad_add_fusion = f32[2,1056,6,64]{1,3,2,0:T(8,128)} fusion(f32[2,1024,6,64]{1,3,2,0:T(8,128)} %get-tuple-element.163, f32[2,1024,6,64]{1,3,2,0:T(8,128)} %get-tuple-element.164, f32[2,1024,6,64]{1,3,2,0:T(8,128)} %get-tuple-element.165, f32[2,1024,6,64]{1,3,2,0:T(8,128)} %get-tuple-element.166, f32[2,1024,6,64]{1,3,2,0:T(8,128)} %get-tuple-element.167, ...), kind=kLoop, calls=%fused_computation.25 | loop fusion | flops 21086208 | bytes 88178688 | tf_op jit(solution)/shard_map/transpose(jvp(vmap()))/add_any | solution.py:85
  665.2 12.1 fusion.12
  691.7 5.0 convolution_bitcast_fusion.1
  706.9 5.2 fusion.74
  712.2 9.6 fusion.175
  721.8 9.7 fusion.172
  734.2 40.9 %all-reduce.75 = (f32[768]{0:T(1024)S(1)}, f32[768]{0:T(1024)S(1)}, f32[768]{0:T(1024)S(1)}, f32[768]{0:T(1024)S(1)}) all-reduce(f32[768]{0:T(1024)S(1)} %copy-done.126, f32[768]{0:T(1024)S(1)} %copy-done.127, f32[768]{0:T(1024)S(1)} %copy-done.124, f32[768]{0:T(1024)S(1)} %copy-done.125), channel_id=9, replica_groups=mesh['dp'=16,'mp'=2] {'dp','mp'}, use_global_device_ids=true, to_apply=%region_65.66.clone | all-reduce | flops 3072 | bytes 24576
  780.4 28.5 %multiply_reduce_fusion.33 = (f32[6]{0:T(128)S(1)}, f32[6]{0:T(128)S(1)}, f32[6]{0:T(128)S(1)}, f32[6]{0:T(128)S(1)}, f32[6]{0:T(128)S(1)}, /*index=5*/f32[6]{0:...) fusion(f32[2,1024,6,64]{1,3,2,0:T(8,128)} %copy-done.4, ...), kind=kLoop, calls=%fused_computation.108 | loop fusion | flops 27525018 | bytes 6300056 | tf_op jit(solution)/shard_map/transpose(jvp(vmap()))/reduce_sum | solution.py:85
  809.1 75.8 %psum.7 = f32[6,33]{0,1:T(8,128)S(1)} all-reduce(f32[6,33]{0,1:T(8,128)S(1)} %pad_add_fusion.7), channel_id=1, replica_groups=mesh['dp'=16,'mp'=2] {'dp'}, use_global_device_ids=true, to_apply=%region_62.63 | all-reduce | flops 198 | bytes 1584 | tf_op jit(solution)/shard_map/psum | solution.py:214
  890.8 66.8 %reduce-scatter.30.cloned.1.call-done = f32[48,384]{1,0:T(8,128)} async-done(((f32[768,384]{1,0:T(8,128)}), f32[48,384]{1,0:T(8,128)}) %reduce-scatter.30.cloned.1.call-update) | async-done | bytes 73744
  957.6 129.3 %reduce-scatter.32.cloned.1.call-done = f32[48,384]{1,0:T(8,128)} async-done(((f32[768,384]{1,0:T(8,128)}), f32[48,384]{1,0:T(8,128)}) %reduce-scatter.32.cloned.1.call-update) | async-done | bytes 73744
  1086.9 104.5 %reduce-scatter.22.cloned.1.call-done = f32[768,24]{0,1:T(8,128)} async-done(((f32[768,768]{0,1:T(8,128)}), f32[768,24]{0,1:T(8,128)}) %reduce-scatter.22.cloned.1.call-update) | async-done | bytes 73744 | tf_op jit(solution)/shard_map/reduce_scatter | solution.py:208
  1191.3 143.0 %reduce-scatter.26.cloned.1.call-done = f32[1536,48]{0,1:T(8,128)} async-done(((f32[1536,768]{0,1:T(8,128)}), f32[1536,48]{0,1:T(8,128)}) %reduce-scatter.26.cloned.1.call-update) | async-done | bytes 294928 | tf_op jit(solution)/shard_map/reduce_scatter | solution.py:205
  1334.3 143.3 %reduce-scatter.24.cloned.1.call-done = f32[48,1536]{1,0:T(8,128)} async-done(((f32[768,1536]{1,0:T(8,128)}), f32[48,1536]{1,0:T(8,128)}) %reduce-scatter.24.cloned.1.call-update) | async-done | bytes 294928 | tf_op jit(solution)/shard_map/reduce_scatter | solution.py:204
  (667 shorter events, 264.5 us)
Async XLA Ops:
  7.2 55.0 %copy-start.204 = (s32[32]{0:T(128)S(1)}, s32[32]{0:T(128)}, u32[]{:S(2)}) copy-start(s32[32]{0:T(128)} %param.26) | copy-start | bytes 388
  7.2 55.1 %copy-start.119 = (bf16[48,384]{1,0:T(8,128)(2,1)S(1)}, bf16[48,384]{1,0:T(8,128)(2,1)}, u32[]{:S(2)}) copy-start(bf16[48,384]{1,0:T(8,128)(2,1)} %param.15) | copy-start | bytes 110596
  7.2 99.1 %copy-start.120 = (bf16[48,384]{1,0:T(8,128)(2,1)S(1)}, bf16[48,384]{1,0:T(8,128)(2,1)}, u32[]{:S(2)}) copy-start(bf16[48,384]{1,0:T(8,128)(2,1)} %param.16) | copy-start | bytes 110596
  7.3 140.2 %copy-start.121 = (bf16[48,384]{1,0:T(8,128)(2,1)S(1)}, bf16[48,384]{1,0:T(8,128)(2,1)}, u32[]{:S(2)}) copy-start(bf16[48,384]{1,0:T(8,128)(2,1)} %param.17) | copy-start | bytes 110596
  7.3 184.5 %all-gather.7.cloned.1.call-start = ((), (), s32[]{:S(2)}) async-start(), calls=%async_computation.11 | async-start | bytes 4718592 | tf_op jit(solution)/shard_map/all_gather | solution.py:129
  8.0 293.3 %all-gather.9.cloned.1.call-start = ((), (), s32[]{:S(2)}) async-start(), calls=%async_computation.12 | async-start | bytes 1216512 | tf_op jit(solution)/shard_map/all_gather | solution.py:118
  8.7 302.8 %all-gather.13.cloned.1.call-start = ((), (), s32[]{:S(2)}) async-start(), calls=%async_computation.14 | async-start | bytes 2506752 | tf_op jit(solution)/shard_map/all_gather | solution.py:114
  62.3 151.3 %copy-start.102 = (pred[2,1024]{1,0:T(4,128)(4,1)}, pred[2,1024]{1,0:T(4,128)(4,1)S(1)}, u32[]{:S(2)}) copy-start(pred[2,1024]{1,0:T(4,128)(4,1)S(1)} %get-tuple-element.190) | copy-start | bytes 6148
  62.4 204.7 %copy-start.94 = (f32[2,1024]{1,0:T(2,128)}, f32[2,1024]{1,0:T(2,128)S(1)}, u32[]{:S(2)}) copy-start(f32[2,1024]{1,0:T(2,128)S(1)} %get-tuple-element.191) | copy-start | bytes 24580
  106.3 94.6 %copy-start.75 = (bf16[768,384]{1,0:T(8,128)(2,1)}, bf16[768,384]{1,0:T(8,128)(2,1)S(1)}, u32[]{:S(2)}) copy-start(bf16[768,384]{1,0:T(8,128)(2,1)S(1)} %all_gather.45) | copy-start | bytes 1769476
  147.4 44.4 %copy-start.77 = (bf16[768,384]{1,0:T(8,128)(2,1)}, bf16[768,384]{1,0:T(8,128)(2,1)S(1)}, u32[]{:S(2)}) copy-start(bf16[768,384]{1,0:T(8,128)(2,1)S(1)} %all_gather.46) | copy-start | bytes 1769476
  216.1 38.6 %copy-start = (f32[2,6,64,1024]{3,2,1,0:T(8,128)}, f32[2,6,64,1024]{3,2,1,0:T(8,128)S(1)}, u32[]{:S(2)}) copy-start(f32[2,6,64,1024]{3,2,1,0:T(8,128)S(1)} %get-tuple-element.195) | copy-start | bytes 9437188
  267.0 30.5 %copy-start.4 = (f32[2,1024,6,64]{1,3,2,0:T(8,128)}, f32[2,1024,6,64]{1,3,2,0:T(8,128)S(1)}, u32[]{:S(2)}) copy-start(f32[2,1024,6,64]{1,3,2,0:T(8,128)S(1)} %copy_multiply_fusion) | copy-start | bytes 9437188
  297.5 6.2 all-to-all-start
  301.2 17.8 %all-gather.11.cloned.1.call-start = ((), (), s32[]{:S(2)}) async-start(), calls=%async_computation.13 | async-start | bytes 4718592 | tf_op jit(solution)/shard_map/all_gather | solution.py:155
  310.9 74.2 %all-gather.15.cloned.1.call-start = ((), (), s32[]{:S(2)}) async-start(), calls=%async_computation.15 | async-start | bytes 2506752 | tf_op jit(solution)/shard_map/all_gather | solution.py:115
  311.5 92.2 %reduce-scatter.16.cloned.1.call-start = ((), (), s32[]{:S(2)}) async-start(), calls=%async_computation.16 | async-start | bytes 4718592 | tf_op jit(solution)/shard_map/reduce_scatter | solution.py:159
  394.2 34.4 %all-gather.17.cloned.1.call-start = ((), (), s32[]{:S(2)}) async-start(), calls=%async_computation.17 | async-start | bytes 4718592 | tf_op jit(solution)/shard_map/all_gather | solution.py:165
  415.1 52.3 %reduce-scatter.18.cloned.1.call-start = ((), (), s32[]{:S(2)}) async-start(), calls=%async_computation.18 | async-start | bytes 4718592 | tf_op jit(solution)/shard_map/reduce_scatter | solution.py:177
  455.1 430.5 %reduce-scatter.20.cloned.1.call-start = ((), (), s32[]{:S(2)}) async-start(), calls=%async_computation.19 | async-start | bytes 4718592 | tf_op jit(solution)/shard_map/reduce_scatter | solution.py:194
  684.1 206.7 %reduce-scatter.28.cloned.1.call-start = ((), (), s32[]{:S(2)}) async-start(), calls=%async_computation.23 | async-start | bytes 1253376
  691.6 266.0 %reduce-scatter.30.cloned.1.call-start = ((), (), s32[]{:S(2)}) async-start(), calls=%async_computation.24 | async-start | bytes 1253376
  699.4 387.5 %reduce-scatter.32.cloned.1.call-start = ((), (), s32[]{:S(2)}) async-start(), calls=%async_computation.25 | async-start | bytes 1253376
  706.9 484.5 %reduce-scatter.22.cloned.1.call-start = ((), (), s32[]{:S(2)}) async-start(), calls=%async_computation.20 | async-start | bytes 2433024 | tf_op jit(solution)/shard_map/reduce_scatter | solution.py:208
  712.1 622.2 %reduce-scatter.26.cloned.1.call-start = ((), (), s32[]{:S(2)}) async-start(), calls=%async_computation.22 | async-start | bytes 5013504 | tf_op jit(solution)/shard_map/reduce_scatter | solution.py:205
  721.8 755.8 %reduce-scatter.24.cloned.1.call-start = ((), (), s32[]{:S(2)}) async-start(), calls=%async_computation.21 | async-start | bytes 5013504 | tf_op jit(solution)/shard_map/reduce_scatter | solution.py:204
  780.3 28.6 %copy-start.187 = (f32[6]{0:T(128)S(1)}, f32[6]{0:T(128)}, u32[]{:S(2)}) copy-start(f32[6]{0:T(128)} %get-tuple-element.85) | copy-start | bytes 76
  780.3 28.6 %copy-start.188 = (f32[6]{0:T(128)S(1)}, f32[6]{0:T(128)}, u32[]{:S(2)}) copy-start(f32[6]{0:T(128)} %get-tuple-element.86) | copy-start | bytes 76
  780.3 28.6 %copy-start.189 = (f32[6]{0:T(128)S(1)}, f32[6]{0:T(128)}, u32[]{:S(2)}) copy-start(f32[6]{0:T(128)} %get-tuple-element.87) | copy-start | bytes 76
  780.3 28.6 %copy-start.190 = (f32[6]{0:T(128)S(1)}, f32[6]{0:T(128)}, u32[]{:S(2)}) copy-start(f32[6]{0:T(128)} %get-tuple-element.88) | copy-start | bytes 76
  780.3 28.6 %copy-start.191 = (f32[6]{0:T(128)S(1)}, f32[6]{0:T(128)}, u32[]{:S(2)}) copy-start(f32[6]{0:T(128)} %get-tuple-element.89) | copy-start | bytes 76
  780.3 28.6 %copy-start.192 = (f32[6]{0:T(128)S(1)}, f32[6]{0:T(128)}, u32[]{:S(2)}) copy-start(f32[6]{0:T(128)} %get-tuple-element.90) | copy-start | bytes 76
  (203 other events, 1192.3 us)
Sparse Core Ops, SparseCore 0:
  9.6 14.8 all-gather.6
  27.4 56.4 all-gather.8
  86.7 69.3 all-gather.12
  311.0 8.0 all-gather.10
  321.7 63.3 all-gather.14
  394.3 9.3 reduce-scatter.15
  415.2 13.3 all-gather.16
  455.2 12.1 reduce-scatter.17
  684.2 12.2 reduce-scatter.19
  701.7 126.3 reduce-scatter.27
  833.4 124.1 reduce-scatter.29
  962.8 124.0 reduce-scatter.31
  1092.7 98.5 reduce-scatter.21
  1196.9 137.3 reduce-scatter.25
  1339.9 137.6 reduce-scatter.23
where the time goes:
time: 1490 us; the launch traced here: 1480 us
  waiting for transfers between devices  658 us (44%)
  blocking collectives  293 us (20%)
  matrix products  288 us (19%)
  other arithmetic  154 us (10%)
  local copies, waits for them, and re-layouts  70.2 us (5%)
  between operations  17.8 us (1%)
    unnamed x18, waiting for transfers between devices  199 us
    reduce_scatter x1, waiting for transfers between devices, on_device(): lax.psum_scatter(expand_grad, 'dp', scatter_dimension=0, tiled=True)  143 us
    reduce_scatter x1, waiting for transfers between devices, on_device(): lax.psum_scatter(shrink_grad, 'dp', scatter_dimension=1, tiled=True)  143 us
    reduce_scatter x1, waiting for transfers between devices, on_device(): lax.psum_scatter(output_grad, ('dp', 'mp'), scatter_dimension=1, tiled=True)  104 us
    unnamed x2, blocking collectives  83 us
    psum x1, blocking collectives, on_device(): taps_grad = lax.psum(taps_grad, 'dp')  75.8 us
    dot_general x6, matrix products, ahead(): return jnp.dot(left, right, preferred_element_type=jnp.float32)  60.9 us
    reduce_sum x4, other arithmetic, nystrom(): mixed = mixed + taps[:, index][None, :, None] * padded[index:index + slots]  46.4 us
  transfers between devices with their start and end apart: 16, of which 11 were waited for; matrix products, arithmetic and copies ran while one was open for 17% of the time, Pallas kernels for 0%

commit v1 on v0

--- a/solution.py
+++ b/solution.py
@@ -8,6 +8,19 @@
 KERNEL = 33
 PINV_STEPS = 6
 HIGH = lax.Precision.HIGHEST
+
+
+def ring_gather(array, axis, dim):
+    peers, mine, width = (lax.axis_size(axis), lax.axis_index(axis), array.shape[dim])
+    ahead = [(i, (i + 1) % peers) for i in range(peers)]
+    out = jnp.zeros((*array.shape[:dim], peers * width, *array.shape[dim + 1 :]), array.dtype)
+    block = array
+    for step in range(peers):
+        holder = (mine - step) % peers
+        out = lax.dynamic_update_slice_in_dim(out, block, holder * width, axis=dim)
+        if step < peers - 1:
+            block = lax.ppermute(block, axis, ahead)
+    return out
 
 
 def ahead(left, right):
@@ -108,7 +121,7 @@
     slots = tokens.shape[0]
     pair = lax.dynamic_slice_in_dim(doc_lengths, group * parts, parts)
     full_query, full_keys, full_values, full_expand, full_shrink = (
-        lax.all_gather(w_query, "dp", axis=0, tiled=True),
+        ring_gather(w_query, "dp", 0),
         lax.all_gather(w_key, "dp", axis=0, tiled=True),
         lax.all_gather(w_value, "dp", axis=0, tiled=True),
         lax.all_gather(w_expand, "dp", axis=0, tiled=True),

time: 1490 us -> 1580 us (1.060)
  waiting for transfers between devices: 658 us -> 751 us
    ppermute x0 -> x15, waiting for transfers between devices: none -> 103 us  [ring_gather(): block = lax.ppermute(block, axis, ahead)]
    unnamed x461 -> x455, local copies, waits for them, and re-layouts: 37.1 us -> 37.4 us
  transfers between devices with their start and end apart: 16 -> 31, of which waited for: 11 -> 24; matrix products, arithmetic and copies ran while one was open for 17% -> 16% of each run, Pallas kernels for 0% -> 0%
where the time goes in v1:
time: 1580 us
  waiting for transfers between devices  751 us (48%)
  blocking collectives  291 us (18%)
  matrix products  284 us (18%)
  other arithmetic  154 us (10%)
  local copies, waits for them, and re-layouts  69.6 us (4%)
  between operations  17.8 us (1%)
    unnamed x18, waiting for transfers between devices  197 us
    reduce_scatter x1, waiting for transfers between devices, on_device(): lax.psum_scatter(expand_grad, 'dp', scatter_dimension=0, tiled=True)  143 us
    reduce_scatter x1, waiting for transfers between devices, on_device(): lax.psum_scatter(shrink_grad, 'dp', scatter_dimension=1, tiled=True)  143 us
    reduce_scatter x1, waiting for transfers between devices, on_device(): lax.psum_scatter(output_grad, ('dp', 'mp'), scatter_dimension=1, tiled=True)  105 us
    ppermute x15, waiting for transfers between devices, ring_gather(): block = lax.ppermute(block, axis, ahead)  103 us
    psum x1, blocking collectives, on_device(): taps_grad = lax.psum(taps_grad, 'dp')  75.2 us
    unnamed x2, blocking collectives  75.2 us
    dot_general x6, matrix products, ahead(): return jnp.dot(left, right, preferred_element_type=jnp.float32)  61.1 us
  transfers between devices with their start and end apart: 31, of which 24 were waited for; matrix products, arithmetic and copies ran while one was open for 16% of the time, Pallas kernels for 0%

profile of v1, /device:TPU:0, one launch (start us, length us, event | category | flops | bytes accessed | tf_op | source)
XLA Modules:
  0.0 1577.0 jit_solution(14431891282919995556)
XLA Ops:
  16.4 47.0 %all_gather.44 = bf16[768,384]{1,0:T(8,128)(2,1)} all-gather(bf16[48,384]{1,0:T(8,128)(2,1)} %param.16), channel_id=1, replica_groups=mesh['dp'=16,'mp'=2] {'dp'}, dimensions={0}, use_global_device_ids=true | all-gather | bytes 626688 | tf_op jit(solution)/shard_map/all_gather | solution.py:125
  63.4 42.3 %all_gather.45 = bf16[768,384]{1,0:T(8,128)(2,1)} all-gather(bf16[48,384]{1,0:T(8,128)(2,1)} %param.17), channel_id=1, replica_groups=mesh['dp'=16,'mp'=2] {'dp'}, dimensions={0}, use_global_device_ids=true | all-gather | bytes 626688 | tf_op jit(solution)/shard_map/all_gather | solution.py:126
  110.0 38.0 %all-reduce.76 = (bf16[768]{0:T(1024)(128)(2,1)S(1)}, bf16[768]{0:T(1024)(128)(2,1)S(1)}, bf16[768]{0:T(1024)(128)(2,1)}, bf16[768]{0:T(1024)(128)(2,1)}) all-reduce(bf16[768]{0:T(1024)(128)(2,1)S(1)} %dynamic-update-slice.1, bf16[768]{0:T(1024)(128)(2,1)S(1)} %dynamic-update-slice, ...), channel_id=1, replica_groups=mesh['dp'=16,'mp'=2] {'dp','mp'}, use_global_device_ids=true, to_apply=%add.68 | all-reduce | flops 3072 | bytes 12288
  156.8 7.5 collective-permute-done.2
  164.4 7.5 collective-permute-done.3
  179.5 7.5 collective-permute-done.5
  187.0 7.7 collective-permute-done.6
  194.7 7.5 collective-permute-done.7
  232.5 7.5 collective-permute-done.12
  240.1 7.5 collective-permute-done.13
  329.5 29.7 %multiply_convert_fusion.1 = bf16[2,1024,6,64]{1,3,2,0:T(8,128)(2,1)} fusion(f32[2,1024,6,64]{1,3,2,0:T(8,128)S(1)} %copy_multiply_fusion, f32[2,6,64,64]{3,2,1,0:T(8,128)S(1)} %fusion.158, f32[6]{0:T(128)S(1)} %copy-done.153, f32[6]{0:T(128)S(1)} %copy-done.180, f32[6]{0:T(128)S(1)} %copy-done.154, f32[6]{0:T(128)S(1)} %copy-done.156, ...), kind=kOutput, calls=%fused_computation.121 | convolution fusion | flops 659816448 | bytes 8168216 | tf_op jit(solution)/shard_map/jvp(vmap(hsj,hjd->shd))/dot_general | solution.py:94
  380.7 35.5 %multiply_convert_fusion = (bf16[2048,1536]{1,0:T(8,128)(2,1)}, f32[2048,1536]{1,0:T(8,128)}, f32[2048,1536]{1,0:T(8,128)}) fusion(bf16[2048,768]{0,1:T(8,128)(2,1)} %all-gather.11.cloned.1.call-done, bf16[768,1536]{1,0:T(8,128)(2,1)} %all-gather.13.cloned.1.call-done), kind=kOutput, calls=%fused_computation.3 | convolution fusion | flops 5036310528 | bytes 36962304 | tf_op jit(solution)/shard_map/dot_general | solution.py:27
  416.2 30.5 %all-gather.15.cloned.1.call-done = bf16[1536,768]{0,1:T(8,128)(2,1)} async-done(((bf16[1536,48]{0,1:T(8,128)(2,1)}), bf16[1536,768]{0,1:T(8,128)(2,1)}) %all-gather.15.cloned.1.call-update) | async-done | bytes 2359312 | tf_op jit(solution)/shard_map/all_gather | solution.py:128
  446.8 9.0 convolution_convert_fusion.1
  476.8 13.5 all-gather.17.cloned.1.call-done
  490.2 17.3 %add_convert_fusion = bf16[2048,1536]{1,0:T(8,128)(2,1)S(1)} fusion(f32[2048,1536]{1,0:T(8,128)} %get-tuple-element.153, f32[2048,1536]{1,0:T(8,128)} %get-tuple-element.200, bf16[2048,768]{0,1:T(8,128)(2,1)} %all-gather.17.cloned.1.call-done, bf16[1536,768]{0,1:T(8,128)(2,1)} %all-gather.15.cloned.1.call-done), kind=kOutput, calls=%fused_computation.2 | convolution fusion | flops 4875878400 | bytes 36962304 | tf_op jit(solution)/shard_map/dot_general | solution.py:31
  517.4 46.4 %all_gather.55 = bf16[768,384]{1,0:T(8,128)(2,1)} all-gather(bf16[48,384]{1,0:T(8,128)(2,1)S(1)} %copy-done.111), channel_id=1, replica_groups=mesh['dp'=16,'mp'=2] {'dp'}, dimensions={0}, use_global_device_ids=true | all-gather | bytes 626688 | tf_op jit(solution)/shard_map/all_gather | solution.py:180
  634.2 15.2 multiply_reduce_fusion.32
  649.6 16.9 %broadcast_multiply_fusion.1 = (f32[2,1024,6,64]{1,3,2,0:T(8,128)}, f32[2,1024,6,64]{1,3,2,0:T(8,128)}, f32[2,1024,6,64]{1,3,2,0:T(8,128)}, f32[2,1024,6,64]{1,3...) fusion(f32[6]{0:T(128)S(1)} %copy-done.181, ...), kind=kLoop, calls=%fused_computation.169 | loop fusion | flops 11796480 | bytes 47194448 | tf_op jit(solution)/shard_map/transpose(jvp(vmap()))/mul | solution.py:98
  666.5 21.3 %broadcast_multiply_fusion = (f32[2,1024,6,64]{1,3,2,0:T(8,128)}, f32[2,1024,6,64]{1,3,2,0:T(8,128)}, f32[2,1024,6,64]{1,3,2,0:T(8,128)}, f32[2,1024,6,64]{1,3,2...) fusion(f32[6]{0:T(128)} %get-tuple-element.134, ...), kind=kLoop, calls=%fused_computation.168 | loop fusion | flops 14155776 | bytes 56631704 | tf_op jit(solution)/shard_map/transpose(jvp(vmap()))/mul | solution.py:98
  727.2 34.6 %pad_add_fusion = f32[2,1056,6,64]{1,3,2,0:T(8,128)} fusion(f32[2,1024,6,64]{1,3,2,0:T(8,128)} %get-tuple-element.163, f32[2,1024,6,64]{1,3,2,0:T(8,128)} %get-tuple-element.164, f32[2,1024,6,64]{1,3,2,0:T(8,128)} %get-tuple-element.165, f32[2,1024,6,64]{1,3,2,0:T(8,128)} %get-tuple-element.166, f32[2,1024,6,64]{1,3,2,0:T(8,128)} %get-tuple-element.167, ...), kind=kLoop, calls=%fused_computation.25 | loop fusion | flops 21086208 | bytes 88178688 | tf_op jit(solution)/shard_map/transpose(jvp(vmap()))/add_any | solution.py:98
  761.8 12.0 fusion.12
  810.9 9.8 fusion.176
  820.8 9.6 fusion.173
  833.0 37.1 %all-reduce.75 = (f32[768]{0:T(1024)S(1)}, f32[768]{0:T(1024)S(1)}, f32[768]{0:T(1024)S(1)}, f32[768]{0:T(1024)S(1)}) all-reduce(f32[768]{0:T(1024)S(1)} %copy-done.126, f32[768]{0:T(1024)S(1)} %copy-done.127, f32[768]{0:T(1024)S(1)} %copy-done.124, f32[768]{0:T(1024)S(1)} %copy-done.125), channel_id=9, replica_groups=mesh['dp'=16,'mp'=2] {'dp','mp'}, use_global_device_ids=true, to_apply=%region_65.66.clone | all-reduce | flops 3072 | bytes 24576
  875.4 28.5 %multiply_reduce_fusion.33 = (f32[6]{0:T(128)S(1)}, f32[6]{0:T(128)S(1)}, f32[6]{0:T(128)S(1)}, f32[6]{0:T(128)S(1)}, f32[6]{0:T(128)S(1)}, /*index=5*/f32[6]{0:...) fusion(f32[2,1024,6,64]{1,3,2,0:T(8,128)} %copy-done.4, ...), kind=kLoop, calls=%fused_computation.108 | loop fusion | flops 27525018 | bytes 6300056 | tf_op jit(solution)/shard_map/transpose(jvp(vmap()))/reduce_sum | solution.py:98
  904.1 75.2 %psum.7 = f32[6,33]{0,1:T(8,128)S(1)} all-reduce(f32[6,33]{0,1:T(8,128)S(1)} %pad_add_fusion.7), channel_id=1, replica_groups=mesh['dp'=16,'mp'=2] {'dp'}, use_global_device_ids=true, to_apply=%region_62.63 | all-reduce | flops 198 | bytes 1584 | tf_op jit(solution)/shard_map/psum | solution.py:227
  985.2 65.3 %reduce-scatter.30.cloned.1.call-done = f32[48,384]{1,0:T(8,128)} async-done(((f32[768,384]{1,0:T(8,128)}), f32[48,384]{1,0:T(8,128)}) %reduce-scatter.30.cloned.1.call-update) | async-done | bytes 73744
  1050.5 129.4 %reduce-scatter.32.cloned.1.call-done = f32[48,384]{1,0:T(8,128)} async-done(((f32[768,384]{1,0:T(8,128)}), f32[48,384]{1,0:T(8,128)}) %reduce-scatter.32.cloned.1.call-update) | async-done | bytes 73744
  1179.9 104.5 %reduce-scatter.22.cloned.1.call-done = f32[768,24]{0,1:T(8,128)} async-done(((f32[768,768]{0,1:T(8,128)}), f32[768,24]{0,1:T(8,128)}) %reduce-scatter.22.cloned.1.call-update) | async-done | bytes 73744 | tf_op jit(solution)/shard_map/reduce_scatter | solution.py:221
  1284.4 142.8 %reduce-scatter.26.cloned.1.call-done = f32[1536,48]{0,1:T(8,128)} async-done(((f32[1536,768]{0,1:T(8,128)}), f32[1536,48]{0,1:T(8,128)}) %reduce-scatter.26.cloned.1.call-update) | async-done | bytes 294928 | tf_op jit(solution)/shard_map/reduce_scatter | solution.py:218
  1427.2 143.1 %reduce-scatter.24.cloned.1.call-done = f32[48,1536]{1,0:T(8,128)} async-done(((f32[768,1536]{1,0:T(8,128)}), f32[48,1536]{1,0:T(8,128)}) %reduce-scatter.24.cloned.1.call-update) | async-done | bytes 294928 | tf_op jit(solution)/shard_map/reduce_scatter | solution.py:217
  (706 shorter events, 351.5 us)
Async XLA Ops:
  7.2 248.0 %all-gather.7.cloned.1.call-start = ((), (), s32[]{:S(2)}) async-start(), calls=%async_computation.11 | async-start | bytes 4718592 | tf_op jit(solution)/shard_map/all_gather | solution.py:142
  8.0 354.9 %all-gather.9.cloned.1.call-start = ((), (), s32[]{:S(2)}) async-start(), calls=%async_computation.12 | async-start | bytes 1216512 | tf_op jit(solution)/shard_map/all_gather | solution.py:131
  8.7 364.4 %all-gather.13.cloned.1.call-start = ((), (), s32[]{:S(2)}) async-start(), calls=%async_computation.14 | async-start | bytes 2506752 | tf_op jit(solution)/shard_map/all_gather | solution.py:127
  8.8 140.5 %collective-permute-start = (bf16[48,384]{1,0:T(8,128)(2,1)}, bf16[48,384]{1,0:T(8,128)(2,1)S(1)}, u32[]{:S(2)}, u32[]{:S(2)}) collective-permute-start(bf16[48,384]{1,0:T(8,128)(2,1)} %param.15), channel_id=1, source_target_pairs={{0,2},{2,4},{4,6},{6,8},{8,10},{10,12},{12,14},{14,16},{16,18},{18... | collective-permute-start | bytes 110600 | tf_op jit(solution)/shard_map/ppermute | solution.py:22
  16.4 312.3 %copy-start.95 = (f32[2,1024]{1,0:T(2,128)}, f32[2,1024]{1,0:T(2,128)S(1)}, u32[]{:S(2)}) copy-start(f32[2,1024]{1,0:T(2,128)S(1)} %get-tuple-element.191) | copy-start | bytes 24580
  149.2 7.6 collective-permute-start.1
  156.8 7.6 collective-permute-start.2
  164.3 7.6 collective-permute-start.3
  171.9 7.6 collective-permute-start.4
  179.5 7.6 collective-permute-start.5
  187.0 7.7 collective-permute-start.6
  194.7 7.6 collective-permute-start.7
  202.3 7.6 collective-permute-start.8
  209.8 7.6 collective-permute-start.9
  217.4 7.6 collective-permute-start.10
  224.9 7.6 collective-permute-start.11
  232.5 7.6 collective-permute-start.12
  240.1 7.6 collective-permute-start.13
  247.6 7.6 collective-permute-start.14
  359.1 6.2 all-to-all-start
  362.8 17.9 %all-gather.11.cloned.1.call-start = ((), (), s32[]{:S(2)}) async-start(), calls=%async_computation.13 | async-start | bytes 4718592 | tf_op jit(solution)/shard_map/all_gather | solution.py:168
  372.5 74.2 %all-gather.15.cloned.1.call-start = ((), (), s32[]{:S(2)}) async-start(), calls=%async_computation.15 | async-start | bytes 2506752 | tf_op jit(solution)/shard_map/all_gather | solution.py:128
  373.1 92.2 %reduce-scatter.16.cloned.1.call-start = ((), (), s32[]{:S(2)}) async-start(), calls=%async_computation.16 | async-start | bytes 4718592 | tf_op jit(solution)/shard_map/reduce_scatter | solution.py:172
  455.8 34.4 %all-gather.17.cloned.1.call-start = ((), (), s32[]{:S(2)}) async-start(), calls=%async_computation.17 | async-start | bytes 4718592 | tf_op jit(solution)/shard_map/all_gather | solution.py:178
  476.7 90.7 %reduce-scatter.18.cloned.1.call-start = ((), (), s32[]{:S(2)}) async-start(), calls=%async_computation.18 | async-start | bytes 4718592 | tf_op jit(solution)/shard_map/reduce_scatter | solution.py:190
  516.7 463.3 %reduce-scatter.20.cloned.1.call-start = ((), (), s32[]{:S(2)}) async-start(), calls=%async_computation.19 | async-start | bytes 4718592 | tf_op jit(solution)/shard_map/reduce_scatter | solution.py:207
  782.5 202.7 %reduce-scatter.28.cloned.1.call-start = ((), (), s32[]{:S(2)}) async-start(), calls=%async_computation.23 | async-start | bytes 1253376
  790.6 259.9 %reduce-scatter.30.cloned.1.call-start = ((), (), s32[]{:S(2)}) async-start(), calls=%async_computation.24 | async-start | bytes 1253376
  798.1 381.8 %reduce-scatter.32.cloned.1.call-start = ((), (), s32[]{:S(2)}) async-start(), calls=%async_computation.25 | async-start | bytes 1253376
  805.6 478.8 %reduce-scatter.22.cloned.1.call-start = ((), (), s32[]{:S(2)}) async-start(), calls=%async_computation.20 | async-start | bytes 2433024 | tf_op jit(solution)/shard_map/reduce_scatter | solution.py:221
  810.9 616.4 %reduce-scatter.26.cloned.1.call-start = ((), (), s32[]{:S(2)}) async-start(), calls=%async_computation.22 | async-start | bytes 5013504 | tf_op jit(solution)/shard_map/reduce_scatter | solution.py:218
  820.7 749.6 %reduce-scatter.24.cloned.1.call-start = ((), (), s32[]{:S(2)}) async-start(), calls=%async_computation.21 | async-start | bytes 5013504 | tf_op jit(solution)/shard_map/reduce_scatter | solution.py:217
  (215 other events, 2833.9 us)
Sparse Core Ops, SparseCore 0:
  9.6 14.8 all-gather.6
  27.3 56.0 all-gather.8
  86.2 62.9 all-gather.12
  372.6 8.0 all-gather.10
  383.3 63.3 all-gather.14
  455.9 9.3 reduce-scatter.15
  476.8 13.3 all-gather.16
  516.8 12.1 reduce-scatter.17
  782.6 6.8 reduce-scatter.19
  794.6 126.3 reduce-scatter.27
  926.4 124.0 reduce-scatter.29
  1055.7 124.1 reduce-scatter.31
  1185.7 98.6 reduce-scatter.21
  1290.0 137.1 reduce-scatter.25
  1432.8 137.4 reduce-scatter.23
